TPU v7x, 256 devices: a whole 4x4x8 slice. The times are simulated.
256 devices in a mesh: dp: 32 (over z_hi, y, core), level: 8 (over x, z_lo).
Axes of the slice: x: 4, y: 4, z: 8 (z_hi: 4, z_lo: 2; z = z_hi * 2 + z_lo), core: 2. Of those that a mesh axis runs over, the one named last changes fastest.
Arguments:
- token_ids: int32 [32, 8, 1536], P('dp', 'level'), may hold values from 0 to 1023
- decoded_mask: int32 [32, 8, 1536], P('dp', 'level'), may hold values 0 or 1
- levels_done: int32 [32], P('dp'), may hold values from 0 to 7
- code_tables: bfloat16 [8, 1024, 1024], P('level'), may hold values from -6 to 6
- mask_vectors: bfloat16 [8, 1024], P('level'), may hold values from -6 to 6
- w_qkv: bfloat16 [3, 1024, 1024], P(None, 'dp', 'level'), may hold values from -6 to 6
- w_out: bfloat16 [1024, 1024], P('level', 'dp'), may hold values from -0.1875 to 0.1875
- w_expand: bfloat16 [1024, 2048], P('dp'), may hold values from -0.1875 to 0.1875
- w_depth: bfloat16 [5, 1024], replicated, may hold values from -2.5 to 2.5
- w_project: bfloat16 [1024, 1024], P('dp'), may hold values from -0.1875 to 0.1875
- level_heads: bfloat16 [8, 1024, 1024], P('level'), may hold values from -0.1875 to 0.1875
Outputs:
- logits: bfloat16 [32, 8, 1536, 1024], P('dp', 'level')
Inputs may be any that keep to these rules, and one draw needn't show every extreme that they name: `levels_done`: levels below it are fully decoded; the level equal to it is the one being decoded.
All inputs are finite; a program needn't handle non-finite values. No bound on the sum of `decoded_mask` on one device may be relied on, other than what follows from the above.
Results may differ from a plain program's by a relative error of at most 0.006.
Values may be sent and summed in bfloat16 or wider, within the bound.
A program may use at most 128 MiB of HBM per device.

v0:
```python
import jax
import jax.numpy as jnp
from jax import lax
from jax.sharding import PartitionSpec as P

HEADS = 16


def copy_for_each(x, axis):
    copies = jnp.broadcast_to(x, (lax.axis_size(axis), *x.shape))
    return lax.all_to_all(copies, axis, split_axis=0, concat_axis=0, tiled=True)


def laid_out(tiles, dim):
    tiles = jnp.moveaxis(tiles, 0, dim)
    dims = tiles.shape
    return tiles.reshape(*dims[:dim], dims[dim] * dims[dim + 1], *dims[dim + 2 :])


def gather_directly(x, axis, dim):
    tiles = copy_for_each(x, axis)
    return laid_out(tiles, dim)


def side_by_side(arrays, axis, dim, along):
    ends, at = ([], 0)
    for a in arrays[:-1]:
        at += a.shape[along]
        ends.append(at)
    both = jnp.concatenate(arrays, axis=along)
    return tuple(jnp.split(lax.all_gather(both, axis, axis=dim, tiled=True), ends, axis=along))


def with_halo(x, sides, width):
    for axis, dim in sides:
        devices, length = (lax.axis_size(axis), x.shape[dim])
        up = [(i, (i + 1) % devices) for i in range(devices - 1)]
        down = [(j, i) for i, j in up]
        last = lax.slice_in_dim(x, length - width, length, axis=dim)
        leading = lax.slice_in_dim(x, 0, width, axis=dim)
        before = lax.ppermute(last, axis, up)
        after = lax.ppermute(leading, axis, down)
        x = jnp.concatenate([before, x, after], axis=dim)
    return x


def layer_norm(values):
    centered = values - jnp.mean(values, axis=-1, keepdims=True)
    variance = jnp.mean(centered * centered, axis=-1, keepdims=True)
    return centered * lax.rsqrt(variance + 1e-05)


def contract_with(left, shard_piece):
    return jnp.dot(left, shard_piece, preferred_element_type=jnp.float32)


def contract_three(left, shard_piece):
    return jnp.einsum("fk,jkc->jfc", left, shard_piece, preferred_element_type=jnp.float32)


def body(
    token_ids,
    decoded_mask,
    levels_done,
    code_tables,
    mask_vectors,
    w_qkv,
    w_out,
    w_expand,
    w_depth,
    w_project,
    level_heads,
):
    frames = token_ids.shape[2]
    model_width = code_tables.shape[2]
    groups = lax.axis_size("level")
    level_index = lax.axis_index("level")
    local_rows = frames // groups
    head_dim = model_width // HEADS
    scale = head_dim ** (-0.5)
    id_row = token_ids[0, 0]
    flag_row = decoded_mask[0, 0]
    done_count = levels_done[0]
    own_table = code_tables[0]
    fill_row = mask_vectors[0].astype(jnp.float32)
    all_live = level_index < done_count
    current = level_index == done_count
    use_token = all_live | current & (flag_row == 1)
    codes = lax.broadcasted_iota(jnp.int32, (frames, own_table.shape[0]), 1)
    onehot = (id_row[:, None] == codes).astype(jnp.bfloat16)
    picked = jnp.dot(onehot, own_table, preferred_element_type=jnp.float32)
    level_terms = (
        jnp.where(use_token[:, None], picked, fill_row[None, :])
        .astype(jnp.bfloat16)
        .reshape(groups, local_rows, model_width)
    )
    received = lax.all_to_all(level_terms, "level", split_axis=0, concat_axis=0, tiled=True)
    own_rows = jnp.sum(received, axis=0, dtype=jnp.float32)
    normed = layer_norm(own_rows).astype(jnp.bfloat16)
    full_columns = gather_directly(w_qkv, "level", 2)
    projected = contract_three(
        normed, lax.all_gather(full_columns, "dp", axis=1, tiled=True)
    ).astype(jnp.bfloat16)
    queries = projected[0].reshape(local_rows, HEADS, head_dim)
    running_max = jnp.full((HEADS, local_rows), -1e30, jnp.float32)
    accumulated = jnp.zeros((local_rows, HEADS, head_dim), jnp.float32)
    key_piece, value_piece = side_by_side((projected[1], projected[2]), "level", 0, 1)
    piece_rows = key_piece.shape[0]
    key_three = key_piece.reshape(piece_rows, HEADS, head_dim)
    value_three = value_piece.reshape(piece_rows, HEADS, head_dim)
    scores = (
        jnp.einsum("qhd,khd->hqk", queries, key_three, preferred_element_type=jnp.float32) * scale
    )
    new_max = jnp.maximum(running_max, jnp.max(scores, axis=-1))
    shrink = jnp.exp(running_max - new_max)
    weights = jnp.exp(scores - new_max[:, :, None])
    weight_sum = jnp.sum(weights, axis=-1)
    added = jnp.einsum(
        "hqk,khd->qhd",
        weights.astype(jnp.bfloat16),
        value_three,
        preferred_element_type=jnp.float32,
    )
    accumulated = accumulated * shrink.T[:, :, None] + added
    running_max, weight_sum, accumulated = (new_max, weight_sum, accumulated)
    attended = (
        (accumulated / weight_sum.T[:, :, None])
        .reshape(local_rows, model_width)
        .astype(jnp.bfloat16)
    )
    out_full = gather_directly(w_out, "level", 0)
    after_attn = own_rows + jnp.dot(
        attended,
        lax.all_gather(out_full, "dp", axis=1, tiled=True),
        preferred_element_type=jnp.float32,
    )
    normed_two = layer_norm(after_attn).astype(jnp.bfloat16)
    gate_linear = contract_with(normed_two, lax.all_gather(w_expand, "dp", axis=0, tiled=True))
    gated = (gate_linear[:, :model_width] * jax.nn.sigmoid(gate_linear[:, model_width:])).astype(
        jnp.bfloat16
    )
    half_width = w_depth.shape[0] // 2
    padded = with_halo(gated, (("level", 0),), half_width)
    conv = jnp.zeros((local_rows, model_width), jnp.float32)
    for tap_index in range(w_depth.shape[0]):
        conv = conv + padded[tap_index : tap_index + local_rows].astype(jnp.float32) * w_depth[
            tap_index
        ].astype(jnp.float32)
    activated = (conv * jax.nn.sigmoid(conv)).astype(jnp.bfloat16)
    after_conv = after_attn + contract_with(
        activated, lax.all_gather(w_project, "dp", axis=0, tiled=True)
    )
    final_norm = layer_norm(after_conv).astype(jnp.bfloat16)
    own_head = level_heads[0]
    logits = jnp.dot(
        lax.all_gather(final_norm, "level", axis=0, tiled=True),
        own_head,
        preferred_element_type=jnp.float32,
    ).astype(jnp.bfloat16)
    return logits[None, None]


def solution(mesh):
    return jax.shard_map(
        body,
        mesh=mesh,
        in_specs=(
            P("dp", "level", None),
            P("dp", "level", None),
            P("dp"),
            P("level", None, None),
            P("level", None),
            P(None, "dp", "level"),
            P("level", "dp"),
            P("dp", None),
            P(),
            P("dp", None),
            P("level", None, None),
        ),
        out_specs=P("dp", "level", None, None),
        check_vma=False,
    )
```

profile of v0, /device:TPU:1, one launch (start us, length us, event | category | flops | bytes accessed | tf_op | source)
XLA Modules:
  0.0 501.6 jit_solution(8657905231968769645)
XLA Ops:
  6.5 0.9 broadcast_in_dim.57
  7.5 11.9 %all_to_all.15 = bf16[8,3,32,128]{3,2,1,0:T(8,128)(2,1)S(1)} all-to-all(bf16[8,3,32,128]{3,2,1,0:T(8,128)(2,1)S(1)} %broadcast_in_dim.57), channel_id=1, replica_groups=mesh['dp'=32,'level'=8] {'level'}, dimensions={0} | all-to-all | bytes 393216 | tf_op jit(solution)/shard_map/all_to_all | solution.py:11
  19.4 0.7 copy_bitcast_fusion
  20.1 0.7 broadcast_in_dim.61
  21.5 0.7 reduce.2
  22.2 0.7 or_reduce_fusion
  22.9 4.3 select_convert_fusion
  27.2 60.7 %all_to_all.16 = bf16[8,192,1024]{2,1,0:T(8,128)(2,1)S(1)} all-to-all(bf16[8,192,1024]{2,1,0:T(8,128)(2,1)S(1)} %bitcast.63), channel_id=1, replica_groups=mesh['dp'=32,'level'=8] {'level'}, dimensions={0} | all-to-all | bytes 6291456 | tf_op jit(solution)/shard_map/all_to_all | solution.py:97
  87.9 1.8 convert_reduce_fusion
  90.0 13.5 %all-gather.7.cloned.1.call-done = bf16[3,1024,1024]{2,1,0:T(8,128)(2,1)} async-done(((bf16[3,32,1024]{2,1,0:T(8,128)(2,1)}), bf16[3,1024,1024]{2,1,0:T(8,128)(2,1)}) %all-gather.7.cloned.1.call-update) | async-done | bytes 6291472 | tf_op jit(solution)/shard_map/all_gather | solution.py:102
  103.5 4.2 fusion.11
  107.8 0.9 pad_maximum_fusion
  108.8 9.0 %all_to_all.17 = bf16[8,128,32]{1,2,0:T(8,128)(2,1)S(1)} all-to-all(bf16[8,128,32]{1,2,0:T(8,128)(2,1)S(1)} %broadcast_in_dim.59), channel_id=1, replica_groups=mesh['dp'=32,'level'=8] {'level'}, dimensions={0} | all-to-all | bytes 131072 | tf_op jit(solution)/shard_map/all_to_all | solution.py:11
  117.8 0.6 copy_bitcast_fusion.1
  119.9 119.0 %all-gather.9.cloned.1.call-done = bf16[1536,2048]{1,0:T(8,128)(2,1)} async-done(((bf16[192,2048]{1,0:T(8,128)(2,1)}), bf16[1536,2048]{1,0:T(8,128)(2,1)}) %all-gather.9.cloned.1.call-update) | async-done | bytes 6291472 | tf_op jit(solution)/shard_map/all_gather | solution.py:31
  238.9 6.3 %fusion.45 = (bf16[1536,1024]{1,0:T(8,128)(2,1)}, bf16[1536,1024]{1,0:T(8,128)(2,1)}) fusion(bf16[1536,2048]{1,0:T(8,128)(2,1)} %all-gather.9.cloned.1.call-done), kind=kLoop, calls=%fused_computation.81 | loop fusion | bytes 12582912 | tf_op jit(solution)/shard_map/split | solution.py:31
  245.2 4.7 copy.27
  249.9 4.7 copy.26
  254.6 11.1 %multiply_reduce_fusion = (f32[16,192]{1,0:T(8,128)S(1)}, f32[16,192,1536]{2,1,0:T(8,128)}) fusion(bf16[192,16,64]{0,2,1:T(8,128)(2,1)S(1)} %bitcast.61, bf16[1536,16,64]{0,2,1:T(8,128)(2,1)} %bitcast.60), kind=kOutput, calls=%fused_computation.1 | convolution fusion | flops 613413888 | bytes 22425600 | tf_op jit(solution)/shard_map/qhd,khd->hqk/dot_general | solution.py:112
  265.7 9.6 %fusion = f32[16,192]{1,0:T(8,128)S(1)} fusion(f32[16,192,1536]{2,1,0:T(8,128)} %get-tuple-element.22, f32[16,192]{1,0:T(8,128)S(1)} %get-tuple-element.20), kind=kLoop, calls=%fused_computation.2 | loop fusion | flops 14152704 | bytes 18898944 | tf_op jit(solution)/shard_map/reduce_sum | solution.py:117
  275.3 11.1 %divide_convert_fusion = bf16[192,16,64]{0,2,1:T(8,128)(2,1)S(1)} fusion(bf16[1536,16,64]{0,2,1:T(8,128)(2,1)} %bitcast.62, f32[16,192,1536]{2,1,0:T(8,128)} %get-tuple-element.22, f32[16,192]{1,0:T(8,128)S(1)} %get-tuple-element.20, f32[192,16]{0,1:T(8,128)S(1)} %bitcast.65, f32[192,16]{0,1:T(8,128)S(1)} %get-tuple-element.19), kind=kOutput, calls=%fused_computation.23 | convolution fusion | flops 618725376 | bytes 22450176 | tf_op jit(solution)/shard_map/hqk,khd->qhd/dot_general | solution.py:118
  286.4 11.3 %all-gather.11.cloned.1.call-done = bf16[1024,1024]{0,1:T(8,128)(2,1)} async-done(((bf16[1024,32]{0,1:T(8,128)(2,1)}), bf16[1024,1024]{0,1:T(8,128)(2,1)}) %all-gather.11.cloned.1.call-update) | async-done | bytes 2097168 | tf_op jit(solution)/shard_map/all_gather | solution.py:134
  297.7 2.5 fusion.48
  300.5 57.0 %all-gather.13.cloned.1.call-done = bf16[1024,2048]{1,0:T(8,128)(2,1)} async-done(((bf16[32,2048]{1,0:T(8,128)(2,1)}), bf16[1024,2048]{1,0:T(8,128)(2,1)}) %all-gather.13.cloned.1.call-update) | async-done | bytes 4194320 | tf_op jit(solution)/shard_map/all_gather | solution.py:138
  357.5 3.2 fusion.29
  360.9 1.3 collective-permute-start.1
  362.2 4.2 collective-permute-start
  366.5 46.3 %all-gather.15.cloned.1.call-done = bf16[1024,1024]{1,0:T(8,128)(2,1)} async-done(((bf16[32,1024]{1,0:T(8,128)(2,1)}), bf16[1024,1024]{1,0:T(8,128)(2,1)}) %all-gather.15.cloned.1.call-update) | async-done | bytes 2097168 | tf_op jit(solution)/shard_map/all_gather | solution.py:151
  412.8 2.7 fusion.49
  415.7 0.9 multiply_convert_fusion
  416.7 70.3 %all-gather.17.cloned.1.call-done = bf16[1536,1024]{1,0:T(8,128)(2,1)} async-done(((bf16[192,1024]{1,0:T(8,128)(2,1)}), bf16[1536,1024]{1,0:T(8,128)(2,1)}) %all-gather.17.cloned.1.call-update) | async-done | bytes 3145744 | tf_op jit(solution)/shard_map/all_gather | solution.py:156
  487.0 7.8 %fusion.7 = bf16[1,1,1536,1024]{3,2,1,0:T(8,128)(2,1)} fusion(bf16[1536,1024]{1,0:T(8,128)(2,1)} %all-gather.17.cloned.1.call-done, bf16[1,1024,1024]{2,1,0:T(8,128)(2,1)} %param.21), kind=kOutput, calls=%fused_computation.13 | convolution fusion | flops 3222798336 | bytes 8388608 | tf_op jit(solution)/shard_map/dot_general | solution.py:155
  (38 shorter events, 2.6 us)
Async XLA Ops:
  6.5 16.4 %copy-start = (bf16[1,1024,1024]{2,1,0:T(8,128)(2,1)S(1)}, bf16[1,1024,1024]{2,1,0:T(8,128)(2,1)}, u32[]{:S(2)}) copy-start(bf16[1,1024,1024]{2,1,0:T(8,128)(2,1)} %param.14) | copy-start | bytes 6291460
  6.5 96.9 %all-gather.7.cloned.1.call-start = ((), (), s32[]{:S(2)}) async-start(), calls=%async_computation.3 | async-start | bytes 6488064 | tf_op jit(solution)/shard_map/all_gather | solution.py:102
  20.1 218.8 %all-gather.9.cloned.1.call-start = ((), (), s32[]{:S(2)}) async-start(), calls=%async_computation.4 | async-start | bytes 7077888 | tf_op jit(solution)/shard_map/all_gather | solution.py:31
  107.7 1.1 copy-start.3
  108.8 189.0 %all-gather.11.cloned.1.call-start = ((), (), s32[]{:S(2)}) async-start(), calls=%async_computation.5 | async-start | bytes 2162688 | tf_op jit(solution)/shard_map/all_gather | solution.py:134
  118.5 239.0 %all-gather.13.cloned.1.call-start = ((), (), s32[]{:S(2)}) async-start(), calls=%async_computation.6 | async-start | bytes 4325376 | tf_op jit(solution)/shard_map/all_gather | solution.py:138
  119.1 293.7 %all-gather.15.cloned.1.call-start = ((), (), s32[]{:S(2)}) async-start(), calls=%async_computation.7 | async-start | bytes 2162688 | tf_op jit(solution)/shard_map/all_gather | solution.py:151
  119.6 367.3 %all-gather.17.cloned.1.call-start = ((), (), s32[]{:S(2)}) async-start(), calls=%async_computation.8 | async-start | bytes 3538944 | tf_op jit(solution)/shard_map/all_gather | solution.py:156
  300.5 66.0 %copy-start.2 = (bf16[5,1024]{1,0:T(8,128)(2,1)S(1)}, bf16[5,1024]{1,0:T(8,128)(2,1)}, u32[]{:S(2)}) copy-start(bf16[5,1024]{1,0:T(8,128)(2,1)} %param.19) | copy-start | bytes 30724
  360.9 51.8 %collective-permute-start.1 = (bf16[2,1024]{1,0:T(2,128)(2,1)S(1)}, bf16[2,1024]{1,0:T(2,128)(2,1)S(1)}, u32[]{:S(2)}, u32[]{:S(2)}) collective-permute-start(bf16[2,1024]{1,0:T(2,128)(2,1)S(1)} %get-tuple-element.13), channel_id=1, source_target_pairs={{1,0},{2,1},{3,2},{4,3},{5,4},{6,5},{7,6},{9,8},{10,9},{11,10},{12... | collective-permute-start | bytes 12296 | tf_op jit(solution)/shard_map/ppermute | solution.py:42
  362.2 50.5 %collective-permute-start = (bf16[2,1024]{1,0:T(2,128)(2,1)S(1)}, bf16[2,1024]{1,0:T(2,128)(2,1)S(1)}, u32[]{:S(2)}, u32[]{:S(2)}) collective-permute-start(bf16[2,1024]{1,0:T(2,128)(2,1)S(1)} %get-tuple-element.12), channel_id=1, source_target_pairs={{0,1},{1,2},{2,3},{3,4},{4,5},{5,6},{6,7},{8,9},{9,10},{10,11},{11... | collective-permute-start | bytes 12296 | tf_op jit(solution)/shard_map/ppermute | solution.py:41
  487.0 7.8 %copy-start.1 = (bf16[1,1024,1024]{2,1,0:T(8,128)(2,1)S(1)}, bf16[1,1024,1024]{2,1,0:T(8,128)(2,1)}, u32[]{:S(2)}) copy-start(bf16[1,1024,1024]{2,1,0:T(8,128)(2,1)} %param.14) | copy-start | bytes 6291460
Sparse Core Ops, SparseCore 0:
  20.2 83.2 all-gather.6
  108.9 129.9 all-gather.8
  241.5 56.1 all-gather.10
  300.1 57.3 all-gather.12
  359.9 52.8 all-gather.14
  416.8 70.1 all-gather.16
where the time goes:
time: 502 us
  waiting for transfers between devices  318 us (63%)
  blocking collectives  81.6 us (16%)
  matrix products  46.9 us (9%)
  local copies, waits for them, and re-layouts  18.2 us (4%)
  other arithmetic  16.4 us (3%)
  between operations  14.3 us (3%)
  starting transfers between devices  5.7 us (1%)
    all_gather x1, waiting for transfers between devices, side_by_side(): lax.all_gather(both, axis, axis=dim, tiled=True)  119 us
    all_gather x1, waiting for transfers between devices, body(): lax.all_gather(final_norm, 'level', axis=0, tiled=True)  70.3 us
    all_to_all x1, blocking collectives, body(): lax.all_to_all(level_terms, 'level', split_axis=0, concat_axis=0, tiled=T...  60.7 us
    all_gather x1, waiting for transfers between devices, body(): lax.all_gather(w_expand, 'dp', axis=0, tiled=True)  57 us
    all_gather x1, waiting for transfers between devices, body(): lax.all_gather(w_project, 'dp', axis=0, tiled=True)  46.3 us
    all_to_all x2, blocking collectives, copy_for_each(): return lax.all_to_all(copies, axis, split_axis=0, concat_axis=0, tiled=True)  20.9 us
    split x3, local copies, waits for them, and re-layouts, side_by_side(): jnp.split(lax.all_gather(both, axis, axis=dim, tiled=True), ends, axis=al...  15.7 us
    all_gather x1, waiting for transfers between devices, body(): lax.all_gather(full_columns, 'dp', axis=1, tiled=True)  13.5 us
  transfers between devices with their start and end apart: 8, of which 6 were waited for; matrix products, arithmetic and copies ran while one was open for 13% of the time, Pallas kernels for 0%

commit v1 on v0

--- a/solution.py
+++ b/solution.py
@@ -153,7 +153,12 @@
     final_norm = layer_norm(after_conv).astype(jnp.bfloat16)
     own_head = level_heads[0]
     logits = jnp.dot(
-        lax.all_gather(final_norm, "level", axis=0, tiled=True),
+        jnp.concatenate(
+            lax.all_to_all(
+                jnp.stack([final_norm] * lax.psum(1, axis_name="level"), axis=0), "level", 0, 0
+            ),
+            axis=0,
+        ),
         own_head,
         preferred_element_type=jnp.float32,
     ).astype(jnp.bfloat16)

time: 502 us -> 470 us (0.936)
  waiting for transfers between devices: 318 us -> 248 us
  blocking collectives: 81.6 us -> 123 us
    all_gather x1 -> x0, waiting for transfers between devices: 70.3 us -> none  [body(): lax.all_gather(final_norm, 'level', axis=0, tiled=True)]
    all_to_all x0 -> x1, blocking collectives: none -> 41.3 us  [body(): lax.all_to_all(jnp.stack([final_norm] * lax.psum(1, axis_name='level'), a...]
  transfers between devices with their start and end apart: 8 -> 7, of which waited for: 6 -> 5; matrix products, arithmetic and copies ran while one was open for 13% -> 13% of each run, Pallas kernels for 0% -> 0%
where the time goes in v1:
time: 470 us; the launch traced here: 469 us
  waiting for transfers between devices  248 us (53%)
  blocking collectives  123 us (26%)
  matrix products  43.8 us (9%)
  local copies, waits for them, and re-layouts  18.6 us (4%)
  other arithmetic  15.6 us (3%)
  between operations  14 us (3%)
  starting transfers between devices  5.66 us (1%)
    all_gather x1, waiting for transfers between devices, side_by_side(): lax.all_gather(both, axis, axis=dim, tiled=True)  119 us
    all_to_all x1, blocking collectives, body(): lax.all_to_all(level_terms, 'level', split_axis=0, concat_axis=0, tiled=T...  60.7 us
    all_gather x1, waiting for transfers between devices, body(): lax.all_gather(w_expand, 'dp', axis=0, tiled=True)  57 us
    all_gather x1, waiting for transfers between devices, body(): lax.all_gather(w_project, 'dp', axis=0, tiled=True)  46.3 us
    all_to_all x1, blocking collectives, body(): lax.all_to_all(jnp.stack([final_norm] * lax.psum(1, axis_name='level'), a...  41.3 us
    all_to_all x2, blocking collectives, copy_for_each(): return lax.all_to_all(copies, axis, split_axis=0, concat_axis=0, tiled=True)  20.9 us
    split x3, local copies, waits for them, and re-layouts, side_by_side(): jnp.split(lax.all_gather(both, axis, axis=dim, tiled=True), ends, axis=al...  15.7 us
    all_gather x1, waiting for transfers between devices, body(): lax.all_gather(full_columns, 'dp', axis=1, tiled=True)  13.5 us
  transfers between devices with their start and end apart: 7, of which 5 were waited for; matrix products, arithmetic and copies ran while one was open for 13% of the time, Pallas kernels for 0%

profile of v1, /device:TPU:1, one launch (start us, length us, event | category | flops | bytes accessed | tf_op | source)
XLA Modules:
  0.0 468.9 jit_solution(3161507719601360348)
XLA Ops:
  6.5 0.9 broadcast_in_dim.57
  7.5 11.9 %all_to_all.20 = bf16[8,3,32,128]{3,2,1,0:T(8,128)(2,1)S(1)} all-to-all(bf16[8,3,32,128]{3,2,1,0:T(8,128)(2,1)S(1)} %broadcast_in_dim.57), channel_id=1, replica_groups=mesh['dp'=32,'level'=8] {'level'}, dimensions={0} | all-to-all | bytes 393216 | tf_op jit(solution)/shard_map/all_to_all | solution.py:11
  19.4 0.7 copy_bitcast_fusion
  20.1 0.7 broadcast_in_dim.61
  21.5 0.7 reduce.2
  22.2 0.7 or_reduce_fusion
  22.9 4.3 select_convert_fusion
  27.2 60.7 %all_to_all.21 = bf16[8,192,1024]{2,1,0:T(8,128)(2,1)S(1)} all-to-all(bf16[8,192,1024]{2,1,0:T(8,128)(2,1)S(1)} %bitcast.64), channel_id=1, replica_groups=mesh['dp'=32,'level'=8] {'level'}, dimensions={0} | all-to-all | bytes 6291456 | tf_op jit(solution)/shard_map/all_to_all | solution.py:97
  87.9 1.8 convert_reduce_fusion
  90.0 13.5 %all-gather.6.cloned.1.call-done = bf16[3,1024,1024]{2,1,0:T(8,128)(2,1)} async-done(((bf16[3,32,1024]{2,1,0:T(8,128)(2,1)}), bf16[3,1024,1024]{2,1,0:T(8,128)(2,1)}) %all-gather.6.cloned.1.call-update) | async-done | bytes 6291472 | tf_op jit(solution)/shard_map/all_gather | solution.py:102
  103.5 4.2 fusion.11
  107.8 0.9 pad_maximum_fusion
  108.8 9.0 %all_to_all.22 = bf16[8,128,32]{1,2,0:T(8,128)(2,1)S(1)} all-to-all(bf16[8,128,32]{1,2,0:T(8,128)(2,1)S(1)} %broadcast_in_dim.59), channel_id=1, replica_groups=mesh['dp'=32,'level'=8] {'level'}, dimensions={0} | all-to-all | bytes 131072 | tf_op jit(solution)/shard_map/all_to_all | solution.py:11
  117.8 0.6 copy_bitcast_fusion.1
  119.1 0.5 all-gather.14.cloned.1.call-update
  119.8 119.1 %all-gather.8.cloned.1.call-done = bf16[1536,2048]{1,0:T(8,128)(2,1)} async-done(((bf16[192,2048]{1,0:T(8,128)(2,1)}), bf16[1536,2048]{1,0:T(8,128)(2,1)}) %all-gather.8.cloned.1.call-update) | async-done | bytes 6291472 | tf_op jit(solution)/shard_map/all_gather | solution.py:31
  238.9 6.3 %fusion.45 = (bf16[1536,1024]{1,0:T(8,128)(2,1)}, bf16[1536,1024]{1,0:T(8,128)(2,1)}) fusion(bf16[1536,2048]{1,0:T(8,128)(2,1)} %all-gather.8.cloned.1.call-done), kind=kLoop, calls=%fused_computation.81 | loop fusion | bytes 12582912 | tf_op jit(solution)/shard_map/split | solution.py:31
  245.2 4.7 %copy.27 = bf16[1536,1024]{0,1:T(8,128)(2,1)} copy(bf16[1536,1024]{1,0:T(8,128)(2,1)} %get-tuple-element.8) | data formatting | bytes 6291456 | tf_op jit(solution)/shard_map/split | solution.py:31
  249.9 4.6 copy.26
  254.6 11.1 %multiply_reduce_fusion = (f32[16,192]{1,0:T(8,128)S(1)}, f32[16,192,1536]{2,1,0:T(8,128)}) fusion(bf16[192,16,64]{0,2,1:T(8,128)(2,1)S(1)} %bitcast.62, bf16[1536,16,64]{0,2,1:T(8,128)(2,1)} %bitcast.61), kind=kOutput, calls=%fused_computation.1 | convolution fusion | flops 613413888 | bytes 22425600 | tf_op jit(solution)/shard_map/qhd,khd->hqk/dot_general | solution.py:112
  265.7 9.6 %fusion = f32[16,192]{1,0:T(8,128)S(1)} fusion(f32[16,192,1536]{2,1,0:T(8,128)} %get-tuple-element.22, f32[16,192]{1,0:T(8,128)S(1)} %get-tuple-element.20), kind=kLoop, calls=%fused_computation.2 | loop fusion | flops 14152704 | bytes 18898944 | tf_op jit(solution)/shard_map/reduce_sum | solution.py:117
  275.3 11.1 %divide_convert_fusion = bf16[192,16,64]{0,2,1:T(8,128)(2,1)S(1)} fusion(bf16[1536,16,64]{0,2,1:T(8,128)(2,1)} %bitcast.63, f32[16,192,1536]{2,1,0:T(8,128)} %get-tuple-element.22, f32[16,192]{1,0:T(8,128)S(1)} %get-tuple-element.20, f32[192,16]{0,1:T(8,128)S(1)} %bitcast.67, f32[192,16]{0,1:T(8,128)S(1)} %get-tuple-element.19), kind=kOutput, calls=%fused_computation.23 | convolution fusion | flops 618725376 | bytes 22450176 | tf_op jit(solution)/shard_map/hqk,khd->qhd/dot_general | solution.py:118
  286.4 11.4 %all-gather.10.cloned.1.call-done = bf16[1024,1024]{0,1:T(8,128)(2,1)} async-done(((bf16[1024,32]{0,1:T(8,128)(2,1)}), bf16[1024,1024]{0,1:T(8,128)(2,1)}) %all-gather.10.cloned.1.call-update) | async-done | bytes 2097168 | tf_op jit(solution)/shard_map/all_gather | solution.py:134
  297.7 2.5 fusion.48
  300.5 57.0 %all-gather.12.cloned.1.call-done = bf16[1024,2048]{1,0:T(8,128)(2,1)} async-done(((bf16[32,2048]{1,0:T(8,128)(2,1)}), bf16[1024,2048]{1,0:T(8,128)(2,1)}) %all-gather.12.cloned.1.call-update) | async-done | bytes 4194320 | tf_op jit(solution)/shard_map/all_gather | solution.py:138
  357.5 3.2 fusion.29
  360.9 1.3 collective-permute-start.1
  362.2 4.2 collective-permute-start
  366.5 46.3 %all-gather.14.cloned.1.call-done = bf16[1024,1024]{1,0:T(8,128)(2,1)} async-done(((bf16[32,1024]{1,0:T(8,128)(2,1)}), bf16[1024,1024]{1,0:T(8,128)(2,1)}) %all-gather.14.cloned.1.call-update) | async-done | bytes 2097168 | tf_op jit(solution)/shard_map/all_gather | solution.py:151
  412.8 2.7 fusion.49
  416.3 41.3 %all_to_all.23 = bf16[8,192,1024]{2,1,0:T(8,128)(2,1)S(1)} all-to-all(bf16[8,192,1024]{2,1,0:T(8,128)(2,1)S(1)} %stack.2), channel_id=1, replica_groups=mesh['dp'=32,'level'=8] {'level'}, dimensions={0} | all-to-all | bytes 6291456 | tf_op jit(solution)/shard_map/all_to_all | solution.py:157
  457.6 4.7 %fusion.7 = bf16[1,1,1536,1024]{3,2,1,0:T(8,128)(2,1)} fusion(bf16[1536,1024]{1,0:T(8,128)(2,1)S(1)} %bitcast.65, bf16[1,1024,1024]{2,1,0:T(8,128)(2,1)S(1)} %copy-done.4), kind=kOutput, calls=%fused_computation.13 | convolution fusion | flops 3222798336 | bytes 8388608 | tf_op jit(solution)/shard_map/dot_general | solution.py:155
  (39 shorter events, 2.6 us)
Async XLA Ops:
  6.5 16.4 %copy-start = (bf16[1,1024,1024]{2,1,0:T(8,128)(2,1)S(1)}, bf16[1,1024,1024]{2,1,0:T(8,128)(2,1)}, u32[]{:S(2)}) copy-start(bf16[1,1024,1024]{2,1,0:T(8,128)(2,1)} %param.14) | copy-start | bytes 6291460
  6.5 96.9 %all-gather.6.cloned.1.call-start = ((), (), s32[]{:S(2)}) async-start(), calls=%async_computation.4 | async-start | bytes 6488064 | tf_op jit(solution)/shard_map/all_gather | solution.py:102
  20.1 218.8 %all-gather.8.cloned.1.call-start = ((), (), s32[]{:S(2)}) async-start(), calls=%async_computation.5 | async-start | bytes 7077888 | tf_op jit(solution)/shard_map/all_gather | solution.py:31
  107.7 1.1 copy-start.3
  108.8 189.0 %all-gather.10.cloned.1.call-start = ((), (), s32[]{:S(2)}) async-start(), calls=%async_computation.6 | async-start | bytes 2162688 | tf_op jit(solution)/shard_map/all_gather | solution.py:134
  118.5 239.0 %all-gather.12.cloned.1.call-start = ((), (), s32[]{:S(2)}) async-start(), calls=%async_computation.7 | async-start | bytes 4325376 | tf_op jit(solution)/shard_map/all_gather | solution.py:138
  119.0 293.7 %all-gather.14.cloned.1.call-start = ((), (), s32[]{:S(2)}) async-start(), calls=%async_computation.8 | async-start | bytes 2162688 | tf_op jit(solution)/shard_map/all_gather | solution.py:151
  300.5 66.0 %copy-start.2 = (bf16[5,1024]{1,0:T(8,128)(2,1)S(1)}, bf16[5,1024]{1,0:T(8,128)(2,1)}, u32[]{:S(2)}) copy-start(bf16[5,1024]{1,0:T(8,128)(2,1)} %param.19) | copy-start | bytes 30724
  360.9 51.8 %collective-permute-start.1 = (bf16[2,1024]{1,0:T(2,128)(2,1)S(1)}, bf16[2,1024]{1,0:T(2,128)(2,1)S(1)}, u32[]{:S(2)}, u32[]{:S(2)}) collective-permute-start(bf16[2,1024]{1,0:T(2,128)(2,1)S(1)} %get-tuple-element.13), channel_id=1, source_target_pairs={{1,0},{2,1},{3,2},{4,3},{5,4},{6,5},{7,6},{9,8},{10,9},{11,10},{12... | collective-permute-start | bytes 12296 | tf_op jit(solution)/shard_map/ppermute | solution.py:42
  362.2 50.5 %collective-permute-start = (bf16[2,1024]{1,0:T(2,128)(2,1)S(1)}, bf16[2,1024]{1,0:T(2,128)(2,1)S(1)}, u32[]{:S(2)}, u32[]{:S(2)}) collective-permute-start(bf16[2,1024]{1,0:T(2,128)(2,1)S(1)} %get-tuple-element.12), channel_id=1, source_target_pairs={{0,1},{1,2},{2,3},{3,4},{4,5},{5,6},{6,7},{8,9},{9,10},{10,11},{11... | collective-permute-start | bytes 12296 | tf_op jit(solution)/shard_map/ppermute | solution.py:41
  416.3 41.3 %copy-start.4 = (bf16[1,1024,1024]{2,1,0:T(8,128)(2,1)S(1)}, bf16[1,1024,1024]{2,1,0:T(8,128)(2,1)}, u32[]{:S(2)}) copy-start(bf16[1,1024,1024]{2,1,0:T(8,128)(2,1)} %param.21) | copy-start | bytes 6291460
  457.6 4.7 %copy-start.1 = (bf16[1,1024,1024]{2,1,0:T(8,128)(2,1)S(1)}, bf16[1,1024,1024]{2,1,0:T(8,128)(2,1)}, u32[]{:S(2)}) copy-start(bf16[1,1024,1024]{2,1,0:T(8,128)(2,1)} %param.14) | copy-start | bytes 6291460
Sparse Core Ops, SparseCore 0:
  20.2 83.2 all-gather.5
  108.9 129.9 all-gather.7
  241.5 56.2 all-gather.9
  300.1 57.2 all-gather.11
  359.9 52.8 all-gather.13
